TPU v7x, 32 devices: a whole 2x2x4 slice. The times are simulated.
32 devices in a mesh: col: 4 (over z), row: 8 (over y, x, core).
Axes of the slice: x: 2, y: 2, z: 4, core: 2. Of those that a mesh axis runs over, the one named last changes fastest.
Arguments:
- img_emb: bfloat16 [16384, 1024], P(('row', 'col'))
- txt_emb: bfloat16 [16384, 1024], P(('row', 'col'))
- log_scale: float32 [], replicated
Outputs:
- output 1: float32 [], replicated
- output 2: bfloat16 [16384, 1024], P(('row', 'col'))
- output 3: bfloat16 [16384, 1024], P(('row', 'col'))
- output 4: float32 [], replicated
All inputs are finite; a program needn't handle non-finite values.
Results may differ from a plain program's by a relative error of at most 0.001.
Values are sent between devices in bfloat16 or wider.
A program may use at most 1 GiB of HBM per device.

v0:
```python
import jax
import jax.numpy as jnp
from jax import lax
from jax.sharding import PartitionSpec as P, NamedSharding


def solution(mesh):
    n_row = mesh.shape["row"]
    n_col = mesh.shape["col"]
    batch_spec = P(("row", "col"), None)
    both_axes = ("row", "col")

    def local_tile(img_loc, txt_loc, log_scale):
        rows_dev = img_loc.shape[0]
        batch_size = rows_dev * n_row * n_col
        inv_count = 1.0 / (2 * batch_size)
        row_id = lax.axis_index("row")
        col_id = lax.axis_index("col")
        logit_scale = jnp.exp(log_scale)
        img_block = lax.all_gather(img_loc, "col", tiled=True)
        txt_block = lax.all_gather(txt_loc, "row", tiled=True)
        logits = logit_scale * jnp.einsum("id,jd->ij", img_block, txt_block, preferred_element_type=jnp.float32)
        row_glob = row_id * (rows_dev * n_col) + jnp.arange(rows_dev * n_col)
        col_pos = jnp.arange(rows_dev * n_row)
        col_glob = ((col_pos // rows_dev) * n_col + col_id) * rows_dev + col_pos % rows_dev
        diag_mask = row_glob[:, None] == col_glob[None, :]
        row_max = jnp.max(logits, axis=1)
        row_exp = jnp.exp(logits - row_max[:, None])
        row_part = jnp.sum(row_exp, axis=1)
        col_max = jnp.max(logits, axis=0)
        col_exp = jnp.exp(logits - col_max[None, :])
        col_part = jnp.sum(col_exp, axis=0)
        row_top = lax.pmax(row_max, "col")
        row_tot = lax.psum(row_part * jnp.exp(row_max - row_top), "col")
        row_lse = row_top + jnp.log(row_tot)
        col_top = lax.pmax(col_max, "row")
        col_tot = lax.psum(col_part * jnp.exp(col_max - col_top), "row")
        col_lse = col_top + jnp.log(col_tot)
        own_block = lax.dynamic_slice(logits, (col_id * rows_dev, row_id * rows_dev), (rows_dev, rows_dev))
        own_diag = jnp.diagonal(own_block)
        own_row_lse = lax.dynamic_slice(row_lse, (col_id * rows_dev,), (rows_dev,))
        own_col_lse = lax.dynamic_slice(col_lse, (row_id * rows_dev,), (rows_dev,))
        loss_part = jnp.sum(own_row_lse + own_col_lse - 2.0 * own_diag)
        total_loss = lax.psum(loss_part, both_axes) * inv_count
        row_factor = jnp.exp(row_max - row_lse) * inv_count
        col_factor = jnp.exp(col_max - col_lse) * inv_count
        grad_tile = row_exp * row_factor[:, None] + col_exp * col_factor[None, :] - jnp.where(diag_mask, 2.0 * inv_count, 0.0)
        d_log_scale = lax.psum(jnp.sum(grad_tile * logits), both_axes)
        grad_bf = grad_tile.astype(jnp.bfloat16)
        img_part = jnp.einsum("ij,jd->id", grad_bf, txt_block, preferred_element_type=jnp.float32)
        img_sum = lax.psum_scatter(img_part, "col", scatter_dimension=0, tiled=True)
        d_img = (logit_scale * img_sum).astype(jnp.bfloat16)
        txt_part = jnp.einsum("ij,id->jd", grad_bf, img_block, preferred_element_type=jnp.float32)
        txt_sum = lax.psum_scatter(txt_part, "row", scatter_dimension=0, tiled=True)
        d_txt = (logit_scale * txt_sum).astype(jnp.bfloat16)
        return total_loss, d_img, d_txt, d_log_scale

    return jax.shard_map(local_tile, mesh=mesh, in_specs=(batch_spec, batch_spec, P()), out_specs=(P(), batch_spec, batch_spec, P()), check_vma=False)
```

profile of v0, /device:TPU:0, one launch (start us, length us, event | category | flops | bytes accessed | tf_op | source)
XLA Modules:
  0.0 578.1 jit_solution(230004587299922486)
XLA Ops:
  7.2 0.0 all-gather.3.cloned.1.call-start
  7.2 0.7 all-gather.3.cloned.1.call-update
  7.9 0.0 all-gather.5.cloned.1.call-start
  7.9 0.7 all-gather.5.cloned.1.call-update
  8.6 0.0 reduce-scatter.3.cloned.1.call-start
  9.4 83.1 %all-gather.3.cloned.1.call-done = bf16[2048,1024]{1,0:T(8,128)(2,1)} async-done(((bf16[512,1024]{1,0:T(8,128)(2,1)}), bf16[2048,1024]{1,0:T(8,128)(2,1)}) %all-gather.3.cloned.1.call-update) | async-done | bytes 4194320 | tf_op jit(solution)/shard_map/all_gather | solution.py:20
  92.5 54.5 %all-gather.5.cloned.1.call-done = bf16[4096,1024]{1,0:T(8,128)(2,1)} async-done(((bf16[512,1024]{1,0:T(8,128)(2,1)}), bf16[4096,1024]{1,0:T(8,128)(2,1)}) %all-gather.5.cloned.1.call-update) | async-done | bytes 8388624 | tf_op jit(solution)/shard_map/all_gather | solution.py:21
  147.0 25.6 %fusion.14 = (f32[2048]{0:T(1024)S(1)}, f32[4096]{0:T(1024)S(1)}, f32[2048,4096]{1,0:T(8,128)}) fusion(bf16[2048,1024]{1,0:T(8,128)(2,1)} %all-gather.3.cloned.1.call-done, bf16[4096,1024]{1,0:T(8,128)(2,1)} %all-gather.5.cloned.1.call-done, f32[]{:T(128)S(6)} %exp.21), kind=kOutput, calls=%fused_computation.35 | convolution fusion | flops 17205028864 | bytes 46161924 | tf_op jit(solution)/shard_map/id,jd->ij/dot_general | solution.py:22
  172.6 23.5 %pmax.15 = f32[4096]{0:T(1024)S(1)} all-reduce(f32[4096]{0:T(1024)S(1)} %get-tuple-element.7), channel_id=1, replica_groups=mesh['col'=4,'row'=8] {'row'}, use_global_device_ids=true, to_apply=%region_5.6 | all-reduce | flops 4096 | bytes 32768 | tf_op jit(solution)/shard_map/pmax | solution.py:36
  196.1 11.8 %pmax.14 = f32[2048]{0:T(1024)S(1)} all-reduce(f32[2048]{0:T(1024)S(1)} %get-tuple-element.6), channel_id=1, replica_groups=mesh['col'=4,'row'=8] {'col'}, use_global_device_ids=true, to_apply=%region_1.2 | all-reduce | flops 2048 | bytes 16384 | tf_op jit(solution)/shard_map/pmax | solution.py:33
  207.9 15.5 %fusion = (f32[2048]{0:T(1024)S(1)}, f32[4096]{0:T(1024)S(1)}) fusion(f32[2048,4096]{1,0:T(8,128)} %get-tuple-element.16, f32[2048]{0:T(1024)S(1)} %get-tuple-element.6, f32[4096]{0:T(1024)S(1)} %get-tuple-element.7), kind=kLoop, calls=%fused_computation.5 | loop fusion | flops 33548288 | bytes 33603584 | tf_op jit(solution)/shard_map/reduce_sum | solution.py:29
  223.4 22.3 %psum.29 = f32[4096]{0:T(1024)S(1)} all-reduce(f32[4096]{0:T(1024)S(1)} %exponential_multiply_fusion.1), channel_id=1, replica_groups=mesh['col'=4,'row'=8] {'row'}, use_global_device_ids=true, to_apply=%region_7.8 | all-reduce | flops 4096 | bytes 32768 | tf_op jit(solution)/shard_map/psum | solution.py:37
  245.8 8.7 %psum.28 = f32[2048]{0:T(1024)S(1)} all-reduce(f32[2048]{0:T(1024)S(1)} %exponential_multiply_fusion.3), channel_id=1, replica_groups=mesh['col'=4,'row'=8] {'col'}, use_global_device_ids=true, to_apply=%region_3.4 | all-reduce | flops 2048 | bytes 16384 | tf_op jit(solution)/shard_map/psum | solution.py:34
  254.5 21.1 %fusion.2 = (bf16[2048,4096]{1,0:T(8,128)(2,1)S(1)}, f32[]{:T(128)}) fusion(f32[2048,4096]{1,0:T(8,128)} %get-tuple-element.16, s32[4096]{0:T(1024)S(1)} %fusion.12, f32[4096]{0:T(1024)S(1)} %get-tuple-element.12, f32[2048]{0:T(1024)S(1)} %get-tuple-element.10, f32[4096]{0:T(1024)S(1)} %get-tuple-element.7, f32[2048]{0:T(1024)S(1)} %get-tuple-element.6, ...), kind=kLoop, calls=%fused_computation.7 | loop fusion | flops 92274688 | bytes 50405380 | tf_op jit(solution)/shard_map/convert_element_type | solution.py:49
  275.6 0.0 copy-start
  275.6 5.7 copy-done
  281.3 22.9 %fusion.15 = f32[2048,1024]{1,0:T(8,128)} fusion(bf16[2048,4096]{1,0:T(8,128)(2,1)S(1)} %get-tuple-element.14, bf16[4096,1024]{1,0:T(8,128)(2,1)} %all-gather.5.cloned.1.call-done), kind=kOutput, calls=%fused_computation.36 | convolution fusion | flops 17179869184 | bytes 33554432 | tf_op jit(solution)/shard_map/ij,jd->id/dot_general | solution.py:50
  304.2 0.0 reduce-scatter.3.cloned.1.call-update
  304.3 0.0 reduce-scatter.5.cloned.1.call-start
  304.3 23.8 %fusion.16 = f32[4096,1024]{1,0:T(8,128)} fusion(bf16[2048,4096]{1,0:T(8,128)(2,1)} %copy-done, bf16[2048,1024]{1,0:T(8,128)(2,1)} %all-gather.3.cloned.1.call-done), kind=kOutput, calls=%fused_computation.37 | convolution fusion | flops 17179869184 | bytes 37748736 | tf_op jit(solution)/shard_map/ij,id->jd/dot_general | solution.py:53
  328.1 0.0 reduce-scatter.5.cloned.1.call-update
  328.1 1.3 dynamic_slice.11
  329.4 4.5 gather_fusion
  334.0 0.7 subtract_reduce_fusion
  334.6 42.9 %all-reduce = (f32[]{:T(128)}, f32[]{:T(128)}) all-reduce(f32[]{:T(128)} %subtract_reduce_fusion, f32[]{:T(128)} %get-tuple-element.15), channel_id=1, replica_groups=mesh['col'=4,'row'=8] {'row','col'}, use_global_device_ids=true, to_apply=%region_9.10 | all-reduce | flops 2 | bytes 16 | tf_op jit(solution)/shard_map/psum | solution.py:44
  378.2 70.3 %reduce-scatter.3.cloned.1.call-done = f32[512,1024]{1,0:T(8,128)} async-done(((f32[2048,1024]{1,0:T(8,128)}), f32[512,1024]{1,0:T(8,128)}) %reduce-scatter.3.cloned.1.call-update) | async-done | bytes 2097168 | tf_op jit(solution)/shard_map/reduce_scatter | solution.py:51
  448.5 2.8 multiply_convert_fusion.1
  451.3 116.3 %reduce-scatter.5.cloned.1.call-done = f32[512,1024]{1,0:T(8,128)} async-done(((f32[4096,1024]{1,0:T(8,128)}), f32[512,1024]{1,0:T(8,128)}) %reduce-scatter.5.cloned.1.call-update) | async-done | bytes 2097168 | tf_op jit(solution)/shard_map/reduce_scatter | solution.py:54
  567.6 2.8 multiply_convert_fusion
  (7 shorter events, 0.1 us)
Async XLA Ops:
  7.2 85.3 %all-gather.3.cloned.1.call-start = ((), (), s32[]{:S(2)}) async-start(), calls=%async_computation.2 | async-start | bytes 5242880 | tf_op jit(solution)/shard_map/all_gather | solution.py:20
  7.9 139.1 %all-gather.5.cloned.1.call-start = ((), (), s32[]{:S(2)}) async-start(), calls=%async_computation.3 | async-start | bytes 9437184 | tf_op jit(solution)/shard_map/all_gather | solution.py:21
  8.6 439.9 %reduce-scatter.3.cloned.1.call-start = ((), (), s32[]{:S(2)}) async-start(), calls=%async_computation.4 | async-start | bytes 10485760 | tf_op jit(solution)/shard_map/reduce_scatter | solution.py:51
  275.6 5.7 copy-start
  304.3 263.3 %reduce-scatter.5.cloned.1.call-start = ((), (), s32[]{:S(2)}) async-start(), calls=%async_computation.5 | async-start | bytes 18874368 | tf_op jit(solution)/shard_map/reduce_scatter | solution.py:54
Sparse Core Ops, SparseCore 0:
  9.5 82.9 all-gather.2
  94.4 52.6 all-gather.4
  304.4 144.0 reduce-scatter.2
  451.9 115.6 reduce-scatter.4
where the time goes:
time: 579 us; the launch traced here: 578 us
  waiting for transfers between devices  326 us (56%)
  blocking collectives  109 us (19%)
  matrix products  72.3 us (12%)
  other arithmetic  42.9 us (7%)
  between operations  16.3 us (3%)
  local copies, waits for them, and re-layouts  11.5 us (2%)
    reduce_scatter x1, waiting for transfers between devices, local_tile(): txt_sum = lax.psum_scatter(txt_part, 'row', scatter_dimension=0, tiled=True)  116 us
    all_gather x1, waiting for transfers between devices, local_tile(): img_block = lax.all_gather(img_loc, 'col', tiled=True)  83.1 us
    reduce_scatter x1, waiting for transfers between devices, local_tile(): img_sum = lax.psum_scatter(img_part, 'col', scatter_dimension=0, tiled=True)  70.3 us
    all_gather x1, waiting for transfers between devices, local_tile(): txt_block = lax.all_gather(txt_loc, 'row', tiled=True)  54.5 us
    psum x1, blocking collectives, local_tile(): total_loss = lax.psum(loss_part, both_axes) * inv_count  42.9 us
    dot_general x1, matrix products, local_tile(): jnp.einsum('id,jd->ij', img_block, txt_block, preferred_element_type=jnp....  25.6 us
    dot_general x1, matrix products, local_tile(): jnp.einsum('ij,id->jd', grad_bf, img_block, preferred_element_type=jnp.fl...  23.8 us
    pmax x1, blocking collectives, local_tile(): col_top = lax.pmax(col_max, 'row')  23.5 us
  transfers between devices with their start and end apart: 4, of which 4 were waited for; matrix products, arithmetic and copies ran while one was open for 6% of the time, Pallas kernels for 0%

commit v1 on v0

v1 whole, which is shorter than its diff:
```python
import functools

import jax
import jax.numpy as jnp
from jax import lax
from jax.experimental import pallas as pl
from jax.experimental.pallas import tpu as pltpu
from jax.sharding import PartitionSpec as P

F32, BF16 = jnp.float32, jnp.bfloat16
MESH_ID = pl.DeviceIdType.MESH
NT = (((1,), (1,)), ((), ()))
TN = (((0,), (0,)), ((), ()))
LOG2E = 1.4426950408889634

ROWS, DIM, CH = 512, 1024, 128
NI, NTX = 4 * ROWS, 8 * ROWS
BLK, PIECE, HALF = 512, 256, 64
QS, TWO = range(4), range(2)
BATCH = 32 * ROWS
INV = 1.0 / (2 * BATCH)


def img_at(slot, k):
    if slot in (1, 2):
        return BLK + (k // 2) * BLK + (2 - slot) * PIECE + (k % 2) * CH
    return slot * BLK + k * CH


def txt_at(slot, k):
    odd = {1: 0, 5: 1, 3: 2, 7: 3}
    if slot in odd:
        return (4 + k) * BLK + odd[slot] * CH
    if slot in (2, 6):
        return 2 * BLK + (k // 2) * BLK + (slot // 4) * PIECE + (k % 2) * CH
    return slot // 4 * BLK + k * CH


def rows_of(start):
    return pl.ds(pl.multiple_of(start, CH), CH)


def at(i):
    return slice(i * CH, i * CH + CH)


def one(i):
    return slice(i, i + 1)


def kernel(
    t_ref, img_ref, txt_ref,
    loss_ref, dimg_ref, dtxt_ref, dt_ref, e_hbm,
    imgs, txts, est, rs, ra, cs, ca, bvec, erow, ecol, grow, gcol,
    xb, rzl, cb, rc, ry, rzh, oimg, otxt,
    rsend, rrecv, csend, crecv, red, redr,
    s_in, s_est, s_erow, s_ecol, s_out,
    ag, sib, row, colm, redm, x3, x2, zls, core, y3, y2, zhs,
):
    a = lax.axis_index("row")
    z = lax.axis_index("col")
    y, x, c = a // 4, (a // 2) % 2, a % 2
    zl, zh = z % 2, z // 2

    def dev(dx=0, dy=0, dc=0, dzl=0, dzh=0):
        yy = (1 - y) if dy else y
        xx = (1 - x) if dx else x
        cc = (1 - c) if dc else c
        l = (1 - zl) if dzl else zl
        h = (1 - zh) if dzh else zh
        return {"row": yy * 4 + xx * 2 + cc, "col": h * 2 + l}

    def row_peer(p):
        return dev(dx=p // 2, dzl=p % 2)

    def col_peer(p):
        return dev(dc=p // 4, dy=(p // 2) % 2, dzh=p % 2)

    ROW_PEERS, COL_PEERS = range(1, 4), range(1, 8)

    def remote(src, dst, sem, to):
        return pltpu.make_async_remote_copy(src_ref=src, dst_ref=dst, send_sem=sem[0], recv_sem=sem[1], device_id=to, device_id_type=MESH_ID)

    def sems(ref, *i):
        return ref.at[(0, *i)], ref.at[(1, *i)]

    in_i = pltpu.make_async_copy(img_ref, imgs.at[pl.ds(0, ROWS), :], s_in.at[0])
    in_t = pltpu.make_async_copy(txt_ref, txts.at[pl.ds(0, ROWS), :], s_in.at[1])
    in_i.start()
    in_t.start()
    barrier = pltpu.get_barrier_semaphore()
    for p in ROW_PEERS:
        pl.semaphore_signal(barrier, inc=1, device_id=row_peer(p), device_id_type=MESH_ID)
    for p in COL_PEERS:
        pl.semaphore_signal(barrier, inc=1, device_id=col_peer(p), device_id_type=MESH_ID)
    in_i.wait()
    in_t.wait()
    pl.semaphore_wait(barrier, 10)

    to_x, to_y, to_c, to_zl, to_zh = dev(dx=1), dev(dy=1), dev(dc=1), dev(dzl=1), dev(dzh=1)

    def gi(src, dst, n, to):
        return lambda k: remote(imgs.at[rows_of(img_at(src, k)), :], imgs.at[rows_of(img_at(dst, k)), :], sems(ag, n, k), to)

    def gt(src, dst, n, to):
        return lambda k: remote(txts.at[rows_of(txt_at(src, k)), :], txts.at[rows_of(txt_at(dst, k)), :], sems(ag, n, k), to)

    g_zl, g_x0, g_x1 = gi(0, 1, 0, to_zl), gi(0, 2, 1, to_x), gi(1, 3, 2, to_x)
    g_zh, g_y0, g_y1 = gt(0, 1, 3, to_zh), gt(0, 2, 4, to_y), gt(1, 3, 5, to_y)

    def g_c(s, k):
        return remote(txts.at[rows_of(txt_at(s, k)), :], txts.at[rows_of(txt_at(s + 4, k)), :], sems(sib, s, k), to_c)

    for k in QS:
        g_zl(k).start()
        g_x0(k).start()
        g_y0(k).start()
        g_c(0, k).start()
    for k in QS:
        g_zh(k).start()

    scale = jnp.exp(jnp.full((1, CH), t_ref[0], F32))
    scale_w = jnp.concatenate([scale] * (BLK // CH), axis=1) * LOG2E

    rs[...] = jnp.zeros_like(rs)
    ra[...] = jnp.zeros_like(ra)
    cs[...] = jnp.zeros_like(cs)
    ca[...] = jnp.zeros_like(ca)

    def est_copy(p, i0, j0):
        i0 = pl.multiple_of(i0, PIECE)
        return pltpu.make_async_copy(est.at[p], e_hbm.at[pl.ds(j0 // CH, BLK // CH), pl.ds(i0, PIECE), :], s_est.at[p])

    def block(i0, j0, rows, p0, used=True):
        i0 = pl.multiple_of(i0, PIECE)
        j0 = pl.multiple_of(j0, BLK)
        pieces = [(p0 + n, n * PIECE) for n in range(rows // PIECE)]
        for p, r in pieces:
            if used is True:
                est_copy(p, i0 + r, j0).wait()
            else:
                @pl.when(used)
                def _():
                    est_copy(p, i0 + r, j0).wait()
        acc = lax.dot_general(imgs[pl.ds(i0, rows), :], txts[pl.ds(j0, BLK), :], NT, preferred_element_type=F32)
        e = jnp.exp2(acc * scale_w)
        ea = e * acc
        parts = [e[:, at(q)] for q in range(BLK // CH)]
        prods = [ea[:, at(q)] for q in range(BLK // CH)]
        for p, r in pieces:
            for q, part in enumerate(parts):
                est[p, q] = part[r:r + PIECE]
        rs[pl.ds(i0, rows), :] += sum(parts[1:], parts[0])
        ra[pl.ds(i0, rows), :] += sum(prods[1:], prods[0])
        cs[:, pl.ds(j0, BLK)] += jnp.sum(e.reshape(rows // 8, 8, BLK), axis=0)
        ca[:, pl.ds(j0, BLK)] += jnp.sum(ea.reshape(rows // 8, 8, BLK), axis=0)
        for p, r in pieces:
            est_copy(p, i0 + r, j0).start()

    def take_texts(k):
        g_zh(k).wait_recv()
        g_y1(k).start()
        g_c(1, k).start()

    def take_last(k):
        g_y1(k).wait_recv()
        g_c(3, k).start()

    def near(s, _):
        @pl.when(s == 0)
        def _():
            for k in QS:
                g_c(0, k).wait_recv()

        @pl.when(s > 0)
        def _():
            for h in TWO:
                k = 2 * (s - 1) + h
                g_zl(k).wait_recv()
                g_x1(k).start()
                g_y0(k).wait_recv()
                g_c(2, k).start()
            for h in TWO:
                k = 2 * (s - 1) + h
                g_x0(k).wait_recv()
                g_c(2, k).wait_recv()

        def body(n, _):
            block(s * BLK, n * BLK, BLK, 0, s + n > 0)
            block(n * BLK, (s + 1) * BLK, BLK, 2, s + n > 0)
            return 0

        lax.fori_loop(0, s + 1, body, 0)
        return 0

    lax.fori_loop(0, 3, near, 0)

    def far(q, _):
        take_last(q)
        take_texts(q + 1)
        g_c(1, q).wait_recv()
        g_c(3, q).wait_recv()
        for m in range(3):
            block(m * BLK, (4 + q) * BLK, BLK, 2 * m, True if m < 2 else q > 0)

        @pl.when(q == 1)
        def _():
            take_texts(3)

        for h in TWO:
            g_x1(2 * q + h).wait_recv()
        for n in QS:
            block(3 * BLK + q * PIECE, n * BLK, PIECE, n)
        return 0

    take_texts(0)
    lax.fori_loop(0, 2, far, 0)
    take_last(2)
    for n in TWO:
        block(3 * BLK, (4 + n) * BLK, BLK, 2 * n)

    def last(q, _):
        @pl.when(q == 3)
        def _():
            take_last(q)

        g_c(1, q).wait_recv()
        g_c(3, q).wait_recv()
        for m in QS:
            block(m * BLK, (4 + q) * BLK, BLK, 2 * m, True if m < 3 else q > 2)
        return 0

    lax.fori_loop(2, 4, last, 0)
    diag = jnp.zeros((CH, 128), F32)
    for k in QS:
        prod = imgs[at(k), :].astype(F32) * txts[at(k), :].astype(F32)
        for q in range(DIM // CH):
            diag += prod[:, at(q)]
    diag = jnp.sum(diag, axis=0, keepdims=True)
    for p in range(8):
        est_copy(p, 0, 0).wait()

    def get_row(slot, k, buf):
        return pltpu.make_async_copy(e_hbm.at[:, rows_of(img_at(slot, k)), :], erow.at[buf], s_erow.at[buf])

    def get_col(slot, k, buf):
        return pltpu.make_async_copy(e_hbm.at[txt_at(slot, k) // CH], ecol.at[buf], s_ecol.at[buf])

    get_row(3, 0, 0).start()
    get_col(7, 0, 0).start()

    for j in range(NTX // CH):
        csend[one(j), :] = jnp.sum(cs[:, at(j)], axis=0, keepdims=True)
    ex_col = [remote(csend, crecv.at[p - 1], sems(colm, p - 1), col_peer(p)) for p in COL_PEERS]
    for copy in ex_col:
        copy.start()
    for i in range(NI // CH):
        rsend[one(i), :] = jnp.sum(rs[at(i), :].T, axis=0, keepdims=True)
    ex_row = [remote(rsend, rrecv.at[p - 1], sems(row, p - 1), row_peer(p)) for p in ROW_PEERS]
    for copy in ex_row:
        copy.start()
    for copy in ex_col:
        copy.wait_recv()

    loss_v = -2.0 * scale * diag
    dt_v = (-2.0 * INV) * scale * diag
    dt_cols = jnp.zeros((8, CH), F32)
    for slot in range(8):
        for k in QS:
            j = txt_at(slot, k) // CH
            tot = csend[one(j), :]
            for p in COL_PEERS:
                tot += crecv[p - 1, one(txt_at(slot ^ p, k) // CH), :]
            if slot == 0:
                loss_v += jnp.log(tot)
            fac = INV / tot
            bvec[:, at(j)] = fac
            dt_cols += fac * ca[:, at(j)]
    for copy in ex_row:
        copy.wait_recv()
    dt_rows = jnp.zeros((CH, CH), F32)
    for slot in QS:
        for k in QS:
            i = img_at(slot, k) // CH
            tot = rsend[one(i), :]
            for p in ROW_PEERS:
                tot += rrecv[p - 1, one(img_at(slot ^ p, k) // CH), :]
            if slot == 0:
                loss_v += jnp.log(tot)
            fac = jnp.broadcast_to(INV / tot, (CH, CH)).T
            rs[at(i), :] = fac
            dt_rows += fac * ra[at(i), :]
    dt_v += scale * (jnp.sum(dt_rows, axis=0, keepdims=True) + jnp.sum(dt_cols, axis=0, keepdims=True))
    red[0] = jnp.concatenate([loss_v, dt_v, jnp.zeros((6, CH), F32)], axis=0)

    red_to = [to_x, to_zl, to_y, to_zh, to_c]
    ex_red = [remote(red.at[i], redr.at[i], sems(redm, i), to) for i, to in enumerate(red_to)]

    def red_step(i):
        ex_red[i].wait()
        red[i + 1] = red[i] + redr[i]
        if i + 1 < len(ex_red):
            ex_red[i + 1].start()

    ex_red[0].start()

    ri = lax.broadcasted_iota(jnp.int32, (CH, CH), 0)
    ci = lax.broadcasted_iota(jnp.int32, (CH, CH), 1)
    eye2 = jnp.where(ri == ci, 2.0 * INV, 0.0).astype(F32)

    def img_chunk(slot, k, buf, after):
        get_row(slot, k, buf).wait()
        after()
        fac = rs[rows_of(img_at(slot, k)), :]
        for j in range(NTX // CH):
            grow[:, at(j)] = (erow[buf, j] * (fac + bvec[:, at(j)])).astype(BF16)
        if slot == 0:
            j0 = pl.multiple_of(k * CH, CH)
            g = erow[buf, k] * (fac + bvec[:, pl.ds(j0, CH)])
            grow[:, pl.ds(j0, CH)] = (g - eye2).astype(BF16)
        return jnp.dot(grow[...], txts[...], preferred_element_type=F32)

    def txt_chunk(slot, k, buf, after):
        get_col(slot, k, buf).wait()
        after()
        b = bvec[:, pl.ds(pl.multiple_of(txt_at(slot, k), CH), CH)]
        gcol[...] = (ecol[buf] * (rs[...] + b)).astype(BF16)
        if slot == 0:
            own = rows_of(k * CH)
            g = ecol[buf, own, :] * (rs[own, :] + b)
            gcol[own, :] = (g - eye2).astype(BF16)
        return lax.dot_general(gcol[...], imgs[...], TN, preferred_element_type=F32)

    def half(h):
        return pl.ds(h * HALF, HALF)

    def c_x3(k, h):
        return remote(xb.at[3, k, half(h)], xb.at[1, k, half(h)], sems(x3, k, h), to_x)

    def c_x2(k):
        return remote(xb.at[2, k], xb.at[0, k], sems(x2, k), to_x)

    def c_zl(k, h):
        return remote(xb.at[1, k, half(h)], rzl.at[k, half(h)], sems(zls, k, h), to_zl)

    core_buf = {7: 0, 5: 1, 6: 0, 4: 1}
    core_prev = {6: 7, 4: 5}

    def c_core(slot, k):
        return remote(cb.at[core_buf[slot], k], rc.at[slot - 4, k], sems(core, slot - 4, k), to_c)

    def c_y3(k, h):
        return remote(rc.at[3, k, half(h)], ry.at[1, k, half(h)], sems(y3, k, h), to_y)

    def c_y2(k):
        return remote(rc.at[2, k], ry.at[0, k], sems(y2, k), to_y)

    def c_zh(k, h):
        return remote(rc.at[1, k, half(h)], rzh.at[k, half(h)], sems(zhs, k, h), to_zh)

    def core_send(slot, k, buf, after):
        p = txt_chunk(slot, k, buf, after)
        if slot in core_prev:
            c_core(core_prev[slot], k).wait_send()
        cb[core_buf[slot], k] = p
        c_core(slot, k).start()

    def when(cond, fetch):
        @pl.when(cond)
        def _():
            fetch().start()

    def step(t, _):
        k = t - 1

        @pl.when(t < 4)
        def _():
            core_send(7, t, 0, lambda: get_col(3, t, 1).start())

            def row_after():
                when(t > 0, lambda: get_row(1, k, (t + 1) % 2))
                when(t == 0, lambda: get_row(3, 1, 1))

            xb[3, t] = img_chunk(3, t, t % 2, row_after)
            for h in TWO:
                c_x3(t, h).start()

            def col_after():
                when(t == 0, lambda: get_col(7, 1, 0))
                when(t > 0, lambda: get_col(5, k, 0))

            p = txt_chunk(3, t, 1, col_after)
            c_core(7, t).wait_recv()
            rc[3, t] += p
            for h in TWO:
                c_y3(t, h).start()

        @pl.when(t > 0)
        def _():
            shift = t // 4
            core_send(5, k, 0, lambda: get_col(1, k, 1).start())
            p = img_chunk(1, k, (t + 1 + shift) % 2, lambda: get_row(2, k, (t + shift) % 2).start())
            for h in TWO:
                c_x3(k, h).wait_recv()
                xb[1, k, half(h)] += p[h * HALF:h * HALF + HALF]
                c_zl(k, h).start()
            p = txt_chunk(1, k, 1, lambda: get_col(6, k, 0).start())
            c_core(5, k).wait_recv()
            for h in TWO:
                c_y3(k, h).wait_recv()
                rc[1, k, half(h)] += p[h * HALF:h * HALF + HALF] + ry[1, k, half(h)]
                c_zh(k, h).start()
            core_send(6, k, 0, lambda: get_col(2, k, 1).start())

            def row_after():
                when(t < 3, lambda: get_row(3, t + 1, (t + 1) % 2))
                when(t == 3, lambda: get_row(1, 3, 0))
                when(t == 4, lambda: get_row(0, 0, 0))

            xb[2, k] = img_chunk(2, k, (t + shift) % 2, row_after)
            c_x2(k).start()

            def col_after():
                when(t < 3, lambda: get_col(7, t + 1, 0))
                when(t == 3, lambda: get_col(5, 3, 0))
                when(t == 4, lambda: get_col(4, 0, 0))

            p = txt_chunk(2, k, 1, col_after)
            c_core(6, k).wait_recv()
            rc[2, k] += p
            c_y2(k).start()
            for i in QS:
                @pl.when(k == i)
                def _():
                    red_step(i)

        return 0

    def close(k, _):
        core_send(4, k, 0, lambda: get_col(0, k, 1).start())
        p = img_chunk(0, k, k % 2, lambda: when(k < 3, lambda: get_row(0, k + 1, (k + 1) % 2)))
        c_x2(k).wait_recv()
        xb[0, k] += p
        p = txt_chunk(0, k, 1, lambda: when(k < 3, lambda: get_col(4, k + 1, 0)))
        c_core(4, k).wait_recv()
        c_y2(k).wait_recv()
        rc[0, k] += p + ry[0, k]
        return 0

    lax.fori_loop(0, 5, step, 0)
    red_step(4)
    lax.fori_loop(0, 4, close, 0)
    loss_ref[0, 0] = jnp.sum(red[5, one(0), :]) * INV
    dt_ref[0, 0] = jnp.sum(red[5, one(1), :])

    wide = jnp.concatenate([scale] * (DIM // CH), axis=1)

    def out(n, k):
        src, dst = ((oimg, dimg_ref), (otxt, dtxt_ref))[n]
        return pltpu.make_async_copy(src.at[rows_of(k * CH), :], dst.at[rows_of(k * CH), :], s_out.at[n, k])

    def finish(k, _):
        for h in TWO:
            c_zl(k, h).wait_recv()
        oimg[rows_of(k * CH), :] = (wide * (xb[0, k] + rzl[k])).astype(BF16)
        out(0, k).start()
        for h in TWO:
            c_zh(k, h).wait_recv()
        otxt[rows_of(k * CH), :] = (wide * (rc[0, k] + rzh[k])).astype(BF16)
        out(1, k).start()
        return 0

    lax.fori_loop(0, 4, finish, 0)

    for copy in ex_col + ex_row:
        copy.wait_send()
    for k in QS:
        for copy in (g_zl, g_zh, g_x0, g_y0, g_x1, g_y1, c_x2, c_y2):
            copy(k).wait_send()
        for s in QS:
            g_c(s, k).wait_send()
        for h in TWO:
            for copy in (c_x3, c_zl, c_y3, c_zh):
                copy(k, h).wait_send()
        for slot in (6, 4):
            c_core(slot, k).wait_send()
        for n in TWO:
            out(n, k).wait()


def solution(mesh):
    spec = P(("row", "col"), None)
    smem = pl.BlockSpec(memory_space=pltpu.SMEM)
    hbm = pl.BlockSpec(memory_space=pl.ANY)
    v = pltpu.VMEM

    def dma(*shape):
        return pltpu.SemaphoreType.DMA(shape)

    chunk = (CH, DIM)
    scratch = [
        v((NI, DIM), BF16), v((NTX, DIM), BF16), v((8, BLK // CH, PIECE, CH), F32),
        v((NI, CH), F32), v((NI, CH), F32), v((8, NTX), F32), v((8, NTX), F32), v((1, NTX), F32),
        v((2, NTX // CH, CH, CH), F32), v((2, NI, CH), F32), v((CH, NTX), BF16), v((NI, CH), BF16),
        v((4, 4, *chunk), F32), v((4, *chunk), F32), v((2, 4, *chunk), F32), v((4, 4, *chunk), F32), v((2, 4, *chunk), F32), v((4, *chunk), F32),
        v((ROWS, DIM), BF16), v((ROWS, DIM), BF16),
        v((NI // CH, CH), F32), v((3, NI // CH, CH), F32), v((NTX // CH, CH), F32), v((7, NTX // CH, CH), F32), v((6, 8, CH), F32), v((5, 8, CH), F32),
        dma(2), dma(8), dma(2), dma(2), dma(2, 4),
        dma(2, 6, 4), dma(2, 4, 4), dma(2, 3), dma(2, 7), dma(2, 5),
        dma(2, 4, 2), dma(2, 4), dma(2, 4, 2), dma(2, 4, 4), dma(2, 4, 2), dma(2, 4), dma(2, 4, 2),
    ]
    shape = jax.ShapeDtypeStruct
    call = pl.pallas_call(
        kernel,
        out_shape=(shape((1, 1), F32), shape((ROWS, DIM), BF16), shape((ROWS, DIM), BF16), shape((1, 1), F32), shape((NTX // CH, NI, CH), F32)),
        in_specs=[smem, hbm, hbm],
        out_specs=(smem, hbm, hbm, smem, hbm),
        scratch_shapes=scratch,
        compiler_params=pltpu.CompilerParams(collective_id=0, has_side_effects=True, vmem_limit_bytes=67043328),
        name="clip",
    )

    def local(img, txt, log_scale):
        loss, d_img, d_txt, dt, _ = call(log_scale.reshape(1), img, txt)
        return loss[0, 0], d_img, d_txt, dt[0, 0]

    return jax.shard_map(local, mesh=mesh, in_specs=(spec, spec, P()), out_specs=(P(), spec, spec, P()), check_vma=False)
```

time: 579 us -> 219 us (0.38)
  waiting for transfers between devices: 326 us -> 0 us
  Pallas kernels: 0 us -> 209 us
  blocking collectives: 109 us -> 0 us
  matrix products: 72.3 us -> 0 us
  other arithmetic: 42.9 us -> 0 us
  between operations: 16.3 us -> 4.81 us
  local copies, waits for them, and re-layouts: 11.5 us -> 4.52 us
    pallas_call x0 -> x1, Pallas kernels: none -> 209 us  [local(): loss, d_img, d_txt, dt, _ = call(log_scale.reshape(1), img, txt)]
    reduce_scatter x2 -> x0, waiting for transfers between devices: 187 us -> none  [the longest x1 116 us: local_tile(): txt_sum = lax.psum_scatter(txt_part, 'row', scatter_dimension=0, tiled=True)]
    all_gather x2 -> x0, waiting for transfers between devices: 138 us -> none  [the longest x1 83.1 us: local_tile(): img_block = lax.all_gather(img_loc, 'col', tiled=True)]
    psum x3 -> x0, blocking collectives: 73.9 us -> none  [the longest x1 42.9 us: local_tile(): total_loss = lax.psum(loss_part, both_axes) * inv_count]
    dot_general x3 -> x0, matrix products: 72.3 us -> none  [the longest x1 25.6 us: local_tile(): jnp.einsum('id,jd->ij', img_block, txt_block, preferred_element_type=jnp....]
    pmax x2 -> x0, blocking collectives: 35.3 us -> none  [the longest x1 23.5 us: local_tile(): col_top = lax.pmax(col_max, 'row')]
    convert_element_type x3 -> x0, other arithmetic: 26.7 us -> none  [the longest x1 21.1 us: local_tile(): grad_bf = grad_tile.astype(jnp.bfloat16)]
    reduce_sum x2 -> x0, other arithmetic: 16.2 us -> none  [the longest x1 15.5 us: local_tile(): row_part = jnp.sum(row_exp, axis=1)]
  transfers between devices with their start and end apart: 4 -> 0, of which waited for: 4 -> 0; matrix products, arithmetic and copies ran while one was open for 6% -> 0% of each run, Pallas kernels for 0% -> 0%
where the time goes in v1:
time: 219 us; the launch traced here: 218 us
  Pallas kernels  209 us (95%)
  between operations  4.81 us (2%)
  local copies, waits for them, and re-layouts  4.52 us (2%)
    pallas_call x1, Pallas kernels, local(): loss, d_img, d_txt, dt, _ = call(log_scale.reshape(1), img, txt)  209 us
    unnamed x2, local copies, waits for them, and re-layouts  4.52 us

profile of v1, /device:TPU:0, one launch (start us, length us, event | category | flops | bytes accessed | tf_op | source)
XLA Modules:
  0.0 218.4 jit_solution(13850244461567154255)
XLA Ops:
  1.3 209.1 %clip.1 = (f32[1,1]{1,0:T(1,128)}, bf16[512,1024]{1,0:T(8,128)(2,1)}, bf16[512,1024]{1,0:T(8,128)(2,1)}, f32[1,1]{1,0:T(1,128)}, f32[32,2048,128]{2,1,0:T(8,128)}) custom-call(f32[1]{0:T(128)} %bitcast.3.t_ref, bf16[512,1024]{1,0:T(8,128)(2,1)} %img_ref.1, bf16[512,1024]{1,0:T(8,128)(2,1)} %txt_ref.1), custom_call_target="tpu_custom_call" | custom-call | tf_op jit(solution)/shard_map/clip/pallas_call | solution.py:524
  211.1 2.3 %copy.13 = bf16[512,1024]{1,0:T(8,128)(2,1)} copy(bf16[512,1024]{1,0:T(8,128)(2,1)} %get-tuple-element.17) | data formatting | bytes 2097152
  213.3 2.3 %copy.14 = bf16[512,1024]{1,0:T(8,128)(2,1)} copy(bf16[512,1024]{1,0:T(8,128)(2,1)} %get-tuple-element.18) | data formatting | bytes 2097152

commit v2 on v1

--- a/solution.py
+++ b/solution.py
@@ -22,18 +22,16 @@
 
 
 def img_at(slot, k):
-    if slot in (1, 2):
-        return BLK + (k // 2) * BLK + (2 - slot) * PIECE + (k % 2) * CH
-    return slot * BLK + k * CH
+    if slot % 2:
+        return 2 * BLK + (k // 2) * BLK + (slot // 2) * PIECE + (k % 2) * CH
+    return slot // 2 * BLK + k * CH
 
 
 def txt_at(slot, k):
-    odd = {1: 0, 5: 1, 3: 2, 7: 3}
-    if slot in odd:
-        return (4 + k) * BLK + odd[slot] * CH
-    if slot in (2, 6):
-        return 2 * BLK + (k // 2) * BLK + (slot // 4) * PIECE + (k % 2) * CH
-    return slot // 4 * BLK + k * CH
+    order = slot % 4 // 2 * 2 + slot // 4
+    if slot % 2:
+        return (4 + k) * BLK + order * CH
+    return order * BLK + k * CH
 
 
 def rows_of(start):
@@ -113,11 +111,10 @@
 
     for k in QS:
         g_zl(k).start()
+        g_zh(k).start()
         g_x0(k).start()
         g_y0(k).start()
         g_c(0, k).start()
-    for k in QS:
-        g_zh(k).start()
 
     scale = jnp.exp(jnp.full((1, CH), t_ref[0], F32))
     scale_w = jnp.concatenate([scale] * (BLK // CH), axis=1) * LOG2E
@@ -131,17 +128,20 @@
         i0 = pl.multiple_of(i0, PIECE)
         return pltpu.make_async_copy(est.at[p], e_hbm.at[pl.ds(j0 // CH, BLK // CH), pl.ds(i0, PIECE), :], s_est.at[p])
 
-    def block(i0, j0, rows, p0, used=True):
-        i0 = pl.multiple_of(i0, PIECE)
-        j0 = pl.multiple_of(j0, BLK)
-        pieces = [(p0 + n, n * PIECE) for n in range(rows // PIECE)]
-        for p, r in pieces:
-            if used is True:
+    def block(m, n, p0, used=True):
+        rows = BLK
+        i0 = pl.multiple_of(m * BLK, BLK)
+        j0 = pl.multiple_of(n * BLK, BLK)
+        pieces = [(p0 + h, h * PIECE) for h in TWO]
+
+        def drained():
+            for p, r in pieces:
                 est_copy(p, i0 + r, j0).wait()
-            else:
-                @pl.when(used)
-                def _():
-                    est_copy(p, i0 + r, j0).wait()
+
+        if used is True:
+            drained()
+        elif used is not False:
+            pl.when(used)(drained)
         acc = lax.dot_general(imgs[pl.ds(i0, rows), :], txts[pl.ds(j0, BLK), :], NT, preferred_element_type=F32)
         e = jnp.exp2(acc * scale_w)
         ea = e * acc
@@ -157,80 +157,90 @@
         for p, r in pieces:
             est_copy(p, i0 + r, j0).start()
 
-    def take_texts(k):
+    def from_zl(k):
+        g_zl(k).wait_recv()
+        g_x1(k).start()
+
+    def from_zh(k):
         g_zh(k).wait_recv()
         g_y1(k).start()
         g_c(1, k).start()
 
-    def take_last(k):
-        g_y1(k).wait_recv()
-        g_c(3, k).start()
-
-    def near(s, _):
-        @pl.when(s == 0)
+    def from_y(s, k):
+        (g_y1 if s else g_y0)(k).wait_recv()
+        g_c(2 + s, k).start()
+
+    def have(n):
+        g_c(1, n).wait_recv()
+        g_c(3, n).wait_recv()
+
+    def near(n, _):
+        @pl.when(n == 0)
         def _():
             for k in QS:
                 g_c(0, k).wait_recv()
 
-        @pl.when(s > 0)
+        @pl.when(n == 1)
         def _():
             for h in TWO:
-                k = 2 * (s - 1) + h
-                g_zl(k).wait_recv()
-                g_x1(k).start()
-                g_y0(k).wait_recv()
-                g_c(2, k).start()
-            for h in TWO:
-                k = 2 * (s - 1) + h
+                from_zl(h)
+                from_y(0, 2 * h)
+                from_zh(h)
+                from_y(0, 2 * h + 1)
+            for k in QS:
                 g_x0(k).wait_recv()
                 g_c(2, k).wait_recv()
 
+        @pl.when(n == 4)
+        def _():
+            from_zl(2)
+            from_y(1, 0)
+            have(0)
+
+        late = (n + 6) // 8
+        block((7 - n) // 6 * n, late * n, 0, n > 0)
+        block((n + 5) // 6, 1 + late * (n - 1), 2, n > 0)
+        return 0
+
+    lax.fori_loop(0, 5, near, 0)
+    from_zh(2)
+    from_y(1, 1)
+    for k in TWO:
+        g_x1(k).wait_recv()
+    have(1)
+
+    def pairs(m):
         def body(n, _):
-            block(s * BLK, n * BLK, BLK, 0, s + n > 0)
-            block(n * BLK, (s + 1) * BLK, BLK, 2, s + n > 0)
+            for h in TWO:
+                block(m, 2 * n + h, 2 * h)
             return 0
 
-        lax.fori_loop(0, s + 1, body, 0)
+        lax.fori_loop(0, 3, body, 0)
+
+    pairs(2)
+    from_zl(3)
+    from_y(1, 2)
+
+    def both(n, _):
+        @pl.when(n == 6)
+        def _():
+            have(2)
+
+        for h in TWO:
+            block(h, n, 2 * h)
         return 0
 
-    lax.fori_loop(0, 3, near, 0)
-
-    def far(q, _):
-        take_last(q)
-        take_texts(q + 1)
-        g_c(1, q).wait_recv()
-        g_c(3, q).wait_recv()
-        for m in range(3):
-            block(m * BLK, (4 + q) * BLK, BLK, 2 * m, True if m < 2 else q > 0)
-
-        @pl.when(q == 1)
-        def _():
-            take_texts(3)
-
-        for h in TWO:
-            g_x1(2 * q + h).wait_recv()
-        for n in QS:
-            block(3 * BLK + q * PIECE, n * BLK, PIECE, n)
-        return 0
-
-    take_texts(0)
-    lax.fori_loop(0, 2, far, 0)
-    take_last(2)
-    for n in TWO:
-        block(3 * BLK, (4 + n) * BLK, BLK, 2 * n)
-
-    def last(q, _):
-        @pl.when(q == 3)
-        def _():
-            take_last(q)
-
-        g_c(1, q).wait_recv()
-        g_c(3, q).wait_recv()
-        for m in QS:
-            block(m * BLK, (4 + q) * BLK, BLK, 2 * m, True if m < 3 else q > 2)
-        return 0
-
-    lax.fori_loop(2, 4, last, 0)
+    lax.fori_loop(5, 7, both, 0)
+    from_zh(3)
+    for k in TWO:
+        g_x1(2 + k).wait_recv()
+    pairs(3)
+    from_y(1, 3)
+    for h in TWO:
+        block(2 + h, 6, 2 * h)
+    have(3)
+    for m in QS:
+        block(m, 7, 2 * m, m < 2)
     diag = jnp.zeros((CH, 128), F32)
     for k in QS:
         prod = imgs[at(k), :].astype(F32) * txts[at(k), :].astype(F32)

time: 219 us -> 197 us (0.90)
  Pallas kernels: 209 us -> 187 us
    pallas_call x1, Pallas kernels: 209 us -> 187 us  [local(): loss, d_img, d_txt, dt, _ = call(log_scale.reshape(1), img, txt)]
where the time goes in v2:
time: 197 us
  Pallas kernels  187 us (95%)
  between operations  4.81 us (2%)
  local copies, waits for them, and re-layouts  4.52 us (2%)
    pallas_call x1, Pallas kernels, local(): loss, d_img, d_txt, dt, _ = call(log_scale.reshape(1), img, txt)  187 us
    unnamed x2, local copies, waits for them, and re-layouts  4.52 us

profile of v2, /device:TPU:0, one launch (start us, length us, event | category | flops | bytes accessed | tf_op | source)
XLA Modules:
  0.0 196.7 jit_solution(4904356556282744164)
XLA Ops:
  1.3 187.3 %clip.1 = (f32[1,1]{1,0:T(1,128)}, bf16[512,1024]{1,0:T(8,128)(2,1)}, bf16[512,1024]{1,0:T(8,128)(2,1)}, f32[1,1]{1,0:T(1,128)}, f32[32,2048,128]{2,1,0:T(8,128)}) custom-call(f32[1]{0:T(128)} %bitcast.3.t_ref, bf16[512,1024]{1,0:T(8,128)(2,1)} %img_ref.1, bf16[512,1024]{1,0:T(8,128)(2,1)} %txt_ref.1), custom_call_target="tpu_custom_call" | custom-call | tf_op jit(solution)/shard_map/clip/pallas_call | solution.py:534
  189.3 2.3 %copy.13 = bf16[512,1024]{1,0:T(8,128)(2,1)} copy(bf16[512,1024]{1,0:T(8,128)(2,1)} %get-tuple-element.17) | data formatting | bytes 2097152
  191.6 2.3 %copy.14 = bf16[512,1024]{1,0:T(8,128)(2,1)} copy(bf16[512,1024]{1,0:T(8,128)(2,1)} %get-tuple-element.18) | data formatting | bytes 2097152

commit v3 on v2

--- a/solution.py
+++ b/solution.py
@@ -15,8 +15,9 @@
 
 ROWS, DIM, CH = 512, 1024, 128
 NI, NTX = 4 * ROWS, 8 * ROWS
-BLK, PIECE, HALF = 512, 256, 64
+BLK, PIECE, CUT = 512, 256, 32
 QS, TWO = range(4), range(2)
+HEAD, TAIL = slice(0, CUT), slice(CUT, CH)
 BATCH = 32 * ROWS
 INV = 1.0 / (2 * BATCH)
 
@@ -50,29 +51,25 @@
     t_ref, img_ref, txt_ref,
     loss_ref, dimg_ref, dtxt_ref, dt_ref, e_hbm,
     imgs, txts, est, rs, ra, cs, ca, bvec, erow, ecol, grow, gcol,
-    xb, rzl, cb, rc, ry, rzh, oimg, otxt,
+    xb, rzl, cb, rc, ry, rzh, oimg, otxt, early, rz,
     rsend, rrecv, csend, crecv, red, redr,
     s_in, s_est, s_erow, s_ecol, s_out,
-    ag, sib, row, colm, redm, x3, x2, zls, core, y3, y2, zhs,
+    ag, sib, row, colm, redm, x3, x2, zls, core, y3, y2, zhs, zf,
 ):
     a = lax.axis_index("row")
     z = lax.axis_index("col")
     y, x, c = a // 4, (a // 2) % 2, a % 2
     zl, zh = z % 2, z // 2
 
-    def dev(dx=0, dy=0, dc=0, dzl=0, dzh=0):
-        yy = (1 - y) if dy else y
-        xx = (1 - x) if dx else x
-        cc = (1 - c) if dc else c
-        l = (1 - zl) if dzl else zl
-        h = (1 - zh) if dzh else zh
+    def dev(*flip):
+        yy, xx, cc, h, l = (1 - v if n in flip else v for n, v in zip(("y", "x", "c", "zh", "zl"), (y, x, c, zh, zl)))
         return {"row": yy * 4 + xx * 2 + cc, "col": h * 2 + l}
 
     def row_peer(p):
-        return dev(dx=p // 2, dzl=p % 2)
+        return dev(*(n for i, n in enumerate(("zl", "x")) if p >> i & 1))
 
     def col_peer(p):
-        return dev(dc=p // 4, dy=(p // 2) % 2, dzh=p % 2)
+        return dev(*(n for i, n in enumerate(("zh", "y", "c")) if p >> i & 1))
 
     ROW_PEERS, COL_PEERS = range(1, 4), range(1, 8)
 
@@ -95,7 +92,7 @@
     in_t.wait()
     pl.semaphore_wait(barrier, 10)
 
-    to_x, to_y, to_c, to_zl, to_zh = dev(dx=1), dev(dy=1), dev(dc=1), dev(dzl=1), dev(dzh=1)
+    to_x, to_y, to_c, to_zl, to_zh = (dev(n) for n in ("x", "y", "c", "zl", "zh"))
 
     def gi(src, dst, n, to):
         return lambda k: remote(imgs.at[rows_of(img_at(src, k)), :], imgs.at[rows_of(img_at(dst, k)), :], sems(ag, n, k), to)
@@ -342,7 +339,7 @@
         return lax.dot_general(gcol[...], imgs[...], TN, preferred_element_type=F32)
 
     def half(h):
-        return pl.ds(h * HALF, HALF)
+        return TAIL if h else HEAD
 
     def c_x3(k, h):
         return remote(xb.at[3, k, half(h)], xb.at[1, k, half(h)], sems(x3, k, h), to_x)
@@ -353,11 +350,8 @@
     def c_zl(k, h):
         return remote(xb.at[1, k, half(h)], rzl.at[k, half(h)], sems(zls, k, h), to_zl)
 
-    core_buf = {7: 0, 5: 1, 6: 0, 4: 1}
-    core_prev = {6: 7, 4: 5}
-
     def c_core(slot, k):
-        return remote(cb.at[core_buf[slot], k], rc.at[slot - 4, k], sems(core, slot - 4, k), to_c)
+        return remote(cb.at[slot - 4], rc.at[slot - 4, k], sems(core, slot - 4, k), to_c)
 
     def c_y3(k, h):
         return remote(rc.at[3, k, half(h)], ry.at[1, k, half(h)], sems(y3, k, h), to_y)
@@ -368,76 +362,125 @@
     def c_zh(k, h):
         return remote(rc.at[1, k, half(h)], rzh.at[k, half(h)], sems(zhs, k, h), to_zh)
 
+    z_first = [remote(xb.at[3, 0, HEAD], rz.at[0], sems(zf, 0), to_zl), remote(rc.at[3, 0, HEAD], rz.at[1], sems(zf, 1), to_zh)]
+
+    def when(cond, go):
+        @pl.when(cond)
+        def _():
+            go()
+
+    def fetch(cond, get):
+        when(cond, lambda: get().start())
+
     def core_send(slot, k, buf, after):
         p = txt_chunk(slot, k, buf, after)
-        if slot in core_prev:
-            c_core(core_prev[slot], k).wait_send()
-        cb[core_buf[slot], k] = p
+        when(k > 0, lambda: c_core(slot, k - 1).wait_send())
+        cb[slot - 4] = p
         c_core(slot, k).start()
-
-    def when(cond, fetch):
-        @pl.when(cond)
-        def _():
-            fetch().start()
 
     def step(t, _):
         k = t - 1
+        km = t - (t + 3) // 4
+        third, shift = t // 3, t // 4
+        at0, at1, at3, at4, on = t == 0, t == 1, t == 3, t == 4, t > 0
 
         @pl.when(t < 4)
         def _():
             core_send(7, t, 0, lambda: get_col(3, t, 1).start())
 
             def row_after():
-                when(t > 0, lambda: get_row(1, k, (t + 1) % 2))
-                when(t == 0, lambda: get_row(3, 1, 1))
-
-            xb[3, t] = img_chunk(3, t, t % 2, row_after)
-            for h in TWO:
-                c_x3(t, h).start()
+                fetch(at1, lambda: get_row(2, 0, 1))
+                fetch(jnp.logical_not(at1), lambda: get_row(1, km, 1 - third))
+
+            xb[3, t] = img_chunk(3, t, third, row_after)
+            when(at0, z_first[0].start)
+            when(on, lambda: c_x3(t, 0).start())
+            c_x3(t, 1).start()
 
             def col_after():
-                when(t == 0, lambda: get_col(7, 1, 0))
-                when(t > 0, lambda: get_col(5, k, 0))
+                fetch(at1, lambda: get_col(6, 0, 0))
+                fetch(jnp.logical_not(at1), lambda: get_col(5, km, 0))
 
             p = txt_chunk(3, t, 1, col_after)
             c_core(7, t).wait_recv()
             rc[3, t] += p
-            for h in TWO:
-                c_y3(t, h).start()
-
-        @pl.when(t > 0)
-        def _():
-            shift = t // 4
-            core_send(5, k, 0, lambda: get_col(1, k, 1).start())
-            p = img_chunk(1, k, (t + 1 + shift) % 2, lambda: get_row(2, k, (t + shift) % 2).start())
-            for h in TWO:
-                c_x3(k, h).wait_recv()
-                xb[1, k, half(h)] += p[h * HALF:h * HALF + HALF]
-                c_zl(k, h).start()
-            p = txt_chunk(1, k, 1, lambda: get_col(6, k, 0).start())
-            c_core(5, k).wait_recv()
-            for h in TWO:
-                c_y3(k, h).wait_recv()
-                rc[1, k, half(h)] += p[h * HALF:h * HALF + HALF] + ry[1, k, half(h)]
-                c_zh(k, h).start()
+            when(at0, z_first[1].start)
+            when(on, lambda: c_y3(t, 0).start())
+            c_y3(t, 1).start()
+
+        @pl.when(jnp.logical_not(at1))
+        def _():
+            core_send(5, km, 0, lambda: get_col(1, km, 1).start())
+
+            def row_after():
+                fetch(at0, lambda: get_row(3, 1, 0))
+                fetch(on, lambda: get_row(2, k, (t + shift) % 2))
+
+            early[...] = img_chunk(1, km, 1 - third, row_after)
+
+            @pl.when(at0)
+            def _():
+                xb[1, 0, HEAD] = early[HEAD]
+                c_zl(0, 0).start()
+
+            def col_after():
+                fetch(at0, lambda: get_col(7, 1, 0))
+                fetch(on, lambda: get_col(6, k, 0))
+
+            p = txt_chunk(1, km, 1, col_after)
+            c_core(5, km).wait_recv()
+            rc[1, km] += p
+            when(at0, lambda: c_zh(0, 0).start())
+
+        def pass_zl(h):
+            c_x3(k, h).wait_recv()
+            xb[1, k, half(h)] += early[half(h)]
+            c_zl(k, h).start()
+
+        def pass_zh(h):
+            c_y3(k, h).wait_recv()
+            rc[1, k, half(h)] += ry[1, k, half(h)]
+            c_zh(k, h).start()
+
+        @pl.when(on)
+        def _():
+            @pl.when(t > 1)
+            def _():
+                pass_zl(0)
+                pass_zh(0)
+
+            pass_zl(1)
+            pass_zh(1)
             core_send(6, k, 0, lambda: get_col(2, k, 1).start())
 
             def row_after():
-                when(t < 3, lambda: get_row(3, t + 1, (t + 1) % 2))
-                when(t == 3, lambda: get_row(1, 3, 0))
-                when(t == 4, lambda: get_row(0, 0, 0))
+                fetch(t < 3, lambda: get_row(3, t + 1, (t + 1) // 3))
+                fetch(at3, lambda: get_row(1, 3, 0))
+                fetch(at4, lambda: get_row(0, 0, 0))
 
             xb[2, k] = img_chunk(2, k, (t + shift) % 2, row_after)
+
+            @pl.when(at1)
+            def _():
+                z_first[0].wait_recv()
+                xb[2, 0, HEAD] += rz[0]
+
             c_x2(k).start()
 
             def col_after():
-                when(t < 3, lambda: get_col(7, t + 1, 0))
-                when(t == 3, lambda: get_col(5, 3, 0))
-                when(t == 4, lambda: get_col(4, 0, 0))
+                fetch(t < 3, lambda: get_col(7, t + 1, 0))
+                fetch(at3, lambda: get_col(5, 3, 0))
+                fetch(at4, lambda: get_col(4, 0, 0))
 
             p = txt_chunk(2, k, 1, col_after)
             c_core(6, k).wait_recv()
             rc[2, k] += p
+
+            @pl.when(at1)
+            def _():
+                z_first[1].wait_recv()
+                rc[2, 0, HEAD] += rz[1]
+
             c_y2(k).start()
             for i in QS:
                 @pl.when(k == i)
@@ -448,10 +491,10 @@
 
     def close(k, _):
         core_send(4, k, 0, lambda: get_col(0, k, 1).start())
-        p = img_chunk(0, k, k % 2, lambda: when(k < 3, lambda: get_row(0, k + 1, (k + 1) % 2)))
+        p = img_chunk(0, k, k % 2, lambda: fetch(k < 3, lambda: get_row(0, k + 1, (k + 1) % 2)))
         c_x2(k).wait_recv()
         xb[0, k] += p
-        p = txt_chunk(0, k, 1, lambda: when(k < 3, lambda: get_col(4, k + 1, 0)))
+        p = txt_chunk(0, k, 1, lambda: fetch(k < 3, lambda: get_col(4, k + 1, 0)))
         c_core(4, k).wait_recv()
         c_y2(k).wait_recv()
         rc[0, k] += p + ry[0, k]
@@ -482,7 +525,7 @@
 
     lax.fori_loop(0, 4, finish, 0)
 
-    for copy in ex_col + ex_row:
+    for copy in ex_col + ex_row + z_first:
         copy.wait_send()
     for k in QS:
         for copy in (g_zl, g_zh, g_x0, g_y0, g_x1, g_y1, c_x2, c_y2):
@@ -490,12 +533,30 @@
         for s in QS:
             g_c(s, k).wait_send()
         for h in TWO:
-            for copy in (c_x3, c_zl, c_y3, c_zh):
-                copy(k, h).wait_send()
-        for slot in (6, 4):
-            c_core(slot, k).wait_send()
+            for copy in (c_zl, c_zh, c_x3, c_y3):
+                if k + h > 0 or copy in (c_zl, c_zh):
+                    copy(k, h).wait_send()
+        c_core(4 + k, 3).wait_send()
         for n in TWO:
             out(n, k).wait()
+
+
+def hand_over(img_ref, txt_ref, dimg_ref, dtxt_ref, buf, sem):
+    parts = [(n, k) for k in TWO for n in TWO]
+
+    def move(n, k, way):
+        here = buf.at[n, pl.ds(k * PIECE, PIECE), :]
+        there = ((img_ref, txt_ref), (dimg_ref, dtxt_ref))[way][n].at[pl.ds(k * PIECE, PIECE), :]
+        src, dst = (here, there) if way else (there, here)
+        return pltpu.make_async_copy(src, dst, sem.at[way, n, k])
+
+    for n, k in parts:
+        move(n, k, 0).start()
+    for n, k in parts:
+        move(n, k, 0).wait()
+        move(n, k, 1).start()
+    for n, k in parts:
+        move(n, k, 1).wait()
 
 
 def solution(mesh):
@@ -512,12 +573,12 @@
         v((NI, DIM), BF16), v((NTX, DIM), BF16), v((8, BLK // CH, PIECE, CH), F32),
         v((NI, CH), F32), v((NI, CH), F32), v((8, NTX), F32), v((8, NTX), F32), v((1, NTX), F32),
         v((2, NTX // CH, CH, CH), F32), v((2, NI, CH), F32), v((CH, NTX), BF16), v((NI, CH), BF16),
-        v((4, 4, *chunk), F32), v((4, *chunk), F32), v((2, 4, *chunk), F32), v((4, 4, *chunk), F32), v((2, 4, *chunk), F32), v((4, *chunk), F32),
-        v((ROWS, DIM), BF16), v((ROWS, DIM), BF16),
+        v((4, 4, *chunk), F32), v((4, *chunk), F32), v((4, *chunk), F32), v((4, 4, *chunk), F32), v((2, 4, *chunk), F32), v((4, *chunk), F32),
+        v((ROWS, DIM), BF16), v((ROWS, DIM), BF16), v(chunk, F32), v((2, CUT, DIM), F32),
         v((NI // CH, CH), F32), v((3, NI // CH, CH), F32), v((NTX // CH, CH), F32), v((7, NTX // CH, CH), F32), v((6, 8, CH), F32), v((5, 8, CH), F32),
         dma(2), dma(8), dma(2), dma(2), dma(2, 4),
         dma(2, 6, 4), dma(2, 4, 4), dma(2, 3), dma(2, 7), dma(2, 5),
-        dma(2, 4, 2), dma(2, 4), dma(2, 4, 2), dma(2, 4, 4), dma(2, 4, 2), dma(2, 4), dma(2, 4, 2),
+        dma(2, 4, 2), dma(2, 4), dma(2, 4, 2), dma(2, 4, 4), dma(2, 4, 2), dma(2, 4), dma(2, 4, 2), dma(2, 2),
     ]
     shape = jax.ShapeDtypeStruct
     call = pl.pallas_call(
@@ -529,9 +590,18 @@
         compiler_params=pltpu.CompilerParams(collective_id=0, has_side_effects=True, vmem_limit_bytes=67043328),
         name="clip",
     )
+    final = pl.pallas_call(
+        hand_over,
+        out_shape=(shape((ROWS, DIM), BF16), shape((ROWS, DIM), BF16)),
+        in_specs=[hbm, hbm],
+        out_specs=(hbm, hbm),
+        scratch_shapes=[v((2, ROWS, DIM), BF16), dma(2, 2, 2)],
+        name="hand_over",
+    )
 
     def local(img, txt, log_scale):
         loss, d_img, d_txt, dt, _ = call(log_scale.reshape(1), img, txt)
+        d_img, d_txt = final(d_img, d_txt)
         return loss[0, 0], d_img, d_txt, dt[0, 0]
 
     return jax.shard_map(local, mesh=mesh, in_specs=(spec, spec, P()), out_specs=(P(), spec, spec, P()), check_vma=False)

time: 197 us -> 188 us (0.954)
  Pallas kernels: 187 us -> 182 us
  local copies, waits for them, and re-layouts: 4.52 us -> 0 us
    pallas_call x1, Pallas kernels: 187 us -> 180 us  [local(): loss, d_img, d_txt, dt, _ = call(log_scale.reshape(1), img, txt)]
    unnamed x2 -> x0, local copies, waits for them, and re-layouts: 4.52 us -> none
    pallas_call x0 -> x1, Pallas kernels: none -> 2.42 us  [local(): d_img, d_txt = final(d_img, d_txt)]
where the time goes in v3:
time: 188 us; the launch traced here: 187 us
  Pallas kernels  182 us (97%)
  between operations  4.75 us (3%)
    pallas_call x1, Pallas kernels, local(): loss, d_img, d_txt, dt, _ = call(log_scale.reshape(1), img, txt)  180 us

profile of v3, /device:TPU:0, one launch (start us, length us, event | category | flops | bytes accessed | tf_op | source)
XLA Modules:
  0.0 187.2 jit_solution(12367917568422955203)
XLA Ops:
  1.3 180.0 %clip.1 = (f32[1,1]{1,0:T(1,128)}, bf16[512,1024]{1,0:T(8,128)(2,1)}, bf16[512,1024]{1,0:T(8,128)(2,1)}, f32[1,1]{1,0:T(1,128)}, f32[32,2048,128]{2,1,0:T(8,128)}) custom-call(f32[1]{0:T(128)} %bitcast.3.t_ref, bf16[512,1024]{1,0:T(8,128)(2,1)} %img_ref.1, bf16[512,1024]{1,0:T(8,128)(2,1)} %txt_ref.1), custom_call_target="tpu_custom_call" | custom-call | tf_op jit(solution)/shard_map/clip/pallas_call | solution.py:603
  181.3 2.4 %hand_over.1 = (bf16[512,1024]{1,0:T(8,128)(2,1)}, bf16[512,1024]{1,0:T(8,128)(2,1)}) custom-call(bf16[512,1024]{1,0:T(8,128)(2,1)} %get-tuple-element.11.img_ref, bf16[512,1024]{1,0:T(8,128)(2,1)} %get-tuple-element.12.txt_ref), custom_call_target="tpu_custom_call" | custom-call | tf_op jit(solution)/shard_map/hand_over/pallas_call | solution.py:604

commit v4 on v3

--- a/solution.py
+++ b/solution.py
@@ -15,9 +15,10 @@
 
 ROWS, DIM, CH = 512, 1024, 128
 NI, NTX = 4 * ROWS, 8 * ROWS
-BLK, PIECE, CUT = 512, 256, 32
+BLK, PIECE, CUTS = 512, 256, (0, 16, 56, CH)
 QS, TWO = range(4), range(2)
-HEAD, TAIL = slice(0, CUT), slice(CUT, CH)
+PARTS = range(3)
+HEAD = slice(0, CUTS[1])
 BATCH = 32 * ROWS
 INV = 1.0 / (2 * BATCH)
 
@@ -339,7 +340,7 @@
         return lax.dot_general(gcol[...], imgs[...], TN, preferred_element_type=F32)
 
     def half(h):
-        return TAIL if h else HEAD
+        return slice(CUTS[h], CUTS[h + 1])
 
     def c_x3(k, h):
         return remote(xb.at[3, k, half(h)], xb.at[1, k, half(h)], sems(x3, k, h), to_x)
@@ -378,6 +379,16 @@
         cb[slot - 4] = p
         c_core(slot, k).start()
 
+    def pass_zl(k, h):
+        c_x3(k, h).wait_recv()
+        xb[1, k, half(h)] += early[half(h)]
+        c_zl(k, h).start()
+
+    def pass_zh(k, h):
+        c_y3(k, h).wait_recv()
+        rc[1, k, half(h)] += ry[1, k, half(h)]
+        c_zh(k, h).start()
+
     def step(t, _):
         k = t - 1
         km = t - (t + 3) // 4
@@ -395,7 +406,8 @@
             xb[3, t] = img_chunk(3, t, third, row_after)
             when(at0, z_first[0].start)
             when(on, lambda: c_x3(t, 0).start())
-            c_x3(t, 1).start()
+            for h in TWO:
+                c_x3(t, h + 1).start()
 
             def col_after():
                 fetch(at1, lambda: get_col(6, 0, 0))
@@ -406,7 +418,8 @@
             rc[3, t] += p
             when(at0, z_first[1].start)
             when(on, lambda: c_y3(t, 0).start())
-            c_y3(t, 1).start()
+            for h in TWO:
+                c_y3(t, h + 1).start()
 
         @pl.when(jnp.logical_not(at1))
         def _():
@@ -432,25 +445,18 @@
             rc[1, km] += p
             when(at0, lambda: c_zh(0, 0).start())
 
-        def pass_zl(h):
-            c_x3(k, h).wait_recv()
-            xb[1, k, half(h)] += early[half(h)]
-            c_zl(k, h).start()
-
-        def pass_zh(h):
-            c_y3(k, h).wait_recv()
-            rc[1, k, half(h)] += ry[1, k, half(h)]
-            c_zh(k, h).start()
+            @pl.when(on)
+            def _():
+                pass_zl(km, 0)
+                pass_zh(km, 0)
+
+            pass_zl(km, 1)
+            pass_zh(km, 1)
 
         @pl.when(on)
         def _():
-            @pl.when(t > 1)
-            def _():
-                pass_zl(0)
-                pass_zh(0)
-
-            pass_zl(1)
-            pass_zh(1)
+            pass_zl(k, 2)
+            pass_zh(k, 2)
             core_send(6, k, 0, lambda: get_col(2, k, 1).start())
 
             def row_after():
@@ -513,17 +519,15 @@
         return pltpu.make_async_copy(src.at[rows_of(k * CH), :], dst.at[rows_of(k * CH), :], s_out.at[n, k])
 
     def finish(k, _):
-        for h in TWO:
+        for h in PARTS:
             c_zl(k, h).wait_recv()
         oimg[rows_of(k * CH), :] = (wide * (xb[0, k] + rzl[k])).astype(BF16)
         out(0, k).start()
-        for h in TWO:
+        for h in PARTS:
             c_zh(k, h).wait_recv()
         otxt[rows_of(k * CH), :] = (wide * (rc[0, k] + rzh[k])).astype(BF16)
         out(1, k).start()
         return 0
-
-    lax.fori_loop(0, 4, finish, 0)
 
     for copy in ex_col + ex_row + z_first:
         copy.wait_send()
@@ -532,11 +536,17 @@
             copy(k).wait_send()
         for s in QS:
             g_c(s, k).wait_send()
-        for h in TWO:
-            for copy in (c_zl, c_zh, c_x3, c_y3):
-                if k + h > 0 or copy in (c_zl, c_zh):
-                    copy(k, h).wait_send()
+        for h in PARTS:
+            if k + h > 0:
+                c_x3(k, h).wait_send()
+                c_y3(k, h).wait_send()
         c_core(4 + k, 3).wait_send()
+    lax.fori_loop(0, 4, finish, 0)
+
+    for k in QS:
+        for h in PARTS:
+            for copy in (c_zl, c_zh):
+                copy(k, h).wait_send()
         for n in TWO:
             out(n, k).wait()
 
@@ -574,11 +584,11 @@
         v((NI, CH), F32), v((NI, CH), F32), v((8, NTX), F32), v((8, NTX), F32), v((1, NTX), F32),
         v((2, NTX // CH, CH, CH), F32), v((2, NI, CH), F32), v((CH, NTX), BF16), v((NI, CH), BF16),
         v((4, 4, *chunk), F32), v((4, *chunk), F32), v((4, *chunk), F32), v((4, 4, *chunk), F32), v((2, 4, *chunk), F32), v((4, *chunk), F32),
-        v((ROWS, DIM), BF16), v((ROWS, DIM), BF16), v(chunk, F32), v((2, CUT, DIM), F32),
+        v((ROWS, DIM), BF16), v((ROWS, DIM), BF16), v(chunk, F32), v((2, CUTS[1], DIM), F32),
         v((NI // CH, CH), F32), v((3, NI // CH, CH), F32), v((NTX // CH, CH), F32), v((7, NTX // CH, CH), F32), v((6, 8, CH), F32), v((5, 8, CH), F32),
         dma(2), dma(8), dma(2), dma(2), dma(2, 4),
         dma(2, 6, 4), dma(2, 4, 4), dma(2, 3), dma(2, 7), dma(2, 5),
-        dma(2, 4, 2), dma(2, 4), dma(2, 4, 2), dma(2, 4, 4), dma(2, 4, 2), dma(2, 4), dma(2, 4, 2), dma(2, 2),
+        dma(2, 4, 3), dma(2, 4), dma(2, 4, 3), dma(2, 4, 4), dma(2, 4, 3), dma(2, 4), dma(2, 4, 3), dma(2, 2),
     ]
     shape = jax.ShapeDtypeStruct
     call = pl.pallas_call(

time: 188 us -> 185 us (0.984)
  Pallas kernels: 182 us -> 180 us
    pallas_call x1, Pallas kernels: 180 us -> 178 us  [local(): loss, d_img, d_txt, dt, _ = call(log_scale.reshape(1), img, txt)]
where the time goes in v4:
time: 185 us
  Pallas kernels  180 us (97%)
  between operations  4.75 us (3%)
    pallas_call x1, Pallas kernels, local(): loss, d_img, d_txt, dt, _ = call(log_scale.reshape(1), img, txt)  178 us

profile of v4, /device:TPU:0, one launch (start us, length us, event | category | flops | bytes accessed | tf_op | source)
XLA Modules:
  0.0 184.8 jit_solution(16435955210012817992)
XLA Ops:
  1.3 177.6 %clip.1 = (f32[1,1]{1,0:T(1,128)}, bf16[512,1024]{1,0:T(8,128)(2,1)}, bf16[512,1024]{1,0:T(8,128)(2,1)}, f32[1,1]{1,0:T(1,128)}, f32[32,2048,128]{2,1,0:T(8,128)}) custom-call(f32[1]{0:T(128)} %bitcast.3.t_ref, bf16[512,1024]{1,0:T(8,128)(2,1)} %img_ref.1, bf16[512,1024]{1,0:T(8,128)(2,1)} %txt_ref.1), custom_call_target="tpu_custom_call" | custom-call | tf_op jit(solution)/shard_map/clip/pallas_call | solution.py:613
  178.9 2.4 %hand_over.1 = (bf16[512,1024]{1,0:T(8,128)(2,1)}, bf16[512,1024]{1,0:T(8,128)(2,1)}) custom-call(bf16[512,1024]{1,0:T(8,128)(2,1)} %get-tuple-element.11.img_ref, bf16[512,1024]{1,0:T(8,128)(2,1)} %get-tuple-element.12.txt_ref), custom_call_target="tpu_custom_call" | custom-call | tf_op jit(solution)/shard_map/hand_over/pallas_call | solution.py:614

commit v5 on v4

--- a/solution.py
+++ b/solution.py
@@ -126,11 +126,10 @@
         i0 = pl.multiple_of(i0, PIECE)
         return pltpu.make_async_copy(est.at[p], e_hbm.at[pl.ds(j0 // CH, BLK // CH), pl.ds(i0, PIECE), :], s_est.at[p])
 
-    def block(m, n, p0, used=True):
-        rows = BLK
-        i0 = pl.multiple_of(m * BLK, BLK)
+    def block(r, n, rows, p0, used=True):
+        i0 = pl.multiple_of(r * PIECE, PIECE)
         j0 = pl.multiple_of(n * BLK, BLK)
-        pieces = [(p0 + h, h * PIECE) for h in TWO]
+        pieces = [(p0 + h, h * PIECE) for h in range(rows // PIECE)]
 
         def drained():
             for p, r in pieces:
@@ -172,6 +171,17 @@
         g_c(1, n).wait_recv()
         g_c(3, n).wait_recv()
 
+    def whole(m, n, p0, used=True):
+        block(2 * m, n, BLK, p0, used)
+
+    def run(r, first, count):
+        def body(i, _):
+            for h in TWO:
+                block(r, 2 * (first + i) + h, PIECE, 2 * (i % 2) + h)
+            return 0
+
+        lax.fori_loop(0, count, body, 0)
+
     def near(n, _):
         @pl.when(n == 0)
         def _():
@@ -189,73 +199,51 @@
                 g_x0(k).wait_recv()
                 g_c(2, k).wait_recv()
 
-        @pl.when(n == 4)
-        def _():
-            from_zl(2)
-            from_y(1, 0)
-            have(0)
-
-        late = (n + 6) // 8
-        block((7 - n) // 6 * n, late * n, 0, n > 0)
-        block((n + 5) // 6, 1 + late * (n - 1), 2, n > 0)
+        late = n // 2
+        whole(n % 2 * (1 - late), late * n, 0, n > 0)
+        whole((n + 2) // 3, 1 + late * (n - 1), 2, n > 0)
         return 0
 
-    lax.fori_loop(0, 5, near, 0)
-    from_zh(2)
-    from_y(1, 1)
-    for k in TWO:
-        g_x1(k).wait_recv()
-    have(1)
-
-    def pairs(m):
-        def body(n, _):
-            for h in TWO:
-                block(m, 2 * n + h, 2 * h)
-            return 0
-
-        lax.fori_loop(0, 3, body, 0)
-
-    pairs(2)
-    from_zl(3)
-    from_y(1, 2)
-
-    def both(n, _):
-        @pl.when(n == 6)
-        def _():
-            have(2)
-
-        for h in TWO:
-            block(h, n, 2 * h)
-        return 0
-
-    lax.fori_loop(5, 7, both, 0)
-    from_zh(3)
-    for k in TWO:
-        g_x1(2 + k).wait_recv()
-    pairs(3)
-    from_y(1, 3)
-    for h in TWO:
-        block(2 + h, 6, 2 * h)
-    have(3)
-    for m in QS:
-        block(m, 7, 2 * m, m < 2)
     diag = jnp.zeros((CH, 128), F32)
     for k in QS:
         prod = imgs[at(k), :].astype(F32) * txts[at(k), :].astype(F32)
         for q in range(DIM // CH):
             diag += prod[:, at(q)]
     diag = jnp.sum(diag, axis=0, keepdims=True)
-    for p in range(8):
-        est_copy(p, 0, 0).wait()
-
-    def get_row(slot, k, buf):
-        return pltpu.make_async_copy(e_hbm.at[:, rows_of(img_at(slot, k)), :], erow.at[buf], s_erow.at[buf])
-
-    def get_col(slot, k, buf):
-        return pltpu.make_async_copy(e_hbm.at[txt_at(slot, k) // CH], ecol.at[buf], s_ecol.at[buf])
-
-    get_row(3, 0, 0).start()
-    get_col(7, 0, 0).start()
+    lax.fori_loop(0, 4, near, 0)
+    run(4, 0, 2)
+    from_zl(2)
+    from_y(1, 0)
+    have(0)
+    for m in TWO:
+        whole(m, 4, 2 * m)
+    from_zh(2)
+    from_y(1, 1)
+    for k in TWO:
+        g_x1(k).wait_recv()
+    run(5, 0, 2)
+    have(1)
+    for m in TWO:
+        whole(2, 4 + m, 2 * m)
+    for m in TWO:
+        whole(m, 5, 2 * m)
+    from_zl(3)
+    from_y(1, 2)
+    run(6, 0, 1)
+    from_zh(3)
+    have(2)
+    for m in range(3):
+        whole(m, 6, 2 * m % 4)
+    run(6, 1, 2)
+    block(6, 6, PIECE, 0)
+    for k in TWO:
+        g_x1(2 + k).wait_recv()
+    from_y(1, 3)
+    run(7, 0, 3)
+    block(7, 6, PIECE, 1)
+    have(3)
+    for m in QS:
+        whole(m, 7, 2 * m, m < 2)
 
     for j in range(NTX // CH):
         csend[one(j), :] = jnp.sum(cs[:, at(j)], axis=0, keepdims=True)
@@ -267,6 +255,18 @@
     ex_row = [remote(rsend, rrecv.at[p - 1], sems(row, p - 1), row_peer(p)) for p in ROW_PEERS]
     for copy in ex_row:
         copy.start()
+
+    for p in range(8):
+        est_copy(p, 0, 0).wait()
+
+    def get_row(slot, k, buf):
+        return pltpu.make_async_copy(e_hbm.at[:, rows_of(img_at(slot, k)), :], erow.at[buf], s_erow.at[buf])
+
+    def get_col(slot, k, buf):
+        return pltpu.make_async_copy(e_hbm.at[txt_at(slot, k) // CH], ecol.at[buf], s_ecol.at[buf])
+
+    get_row(3, 0, 0).start()
+    get_col(7, 0, 0).start()
     for copy in ex_col:
         copy.wait_recv()
 
@@ -578,17 +578,25 @@
     def dma(*shape):
         return pltpu.SemaphoreType.DMA(shape)
 
-    chunk = (CH, DIM)
+    def both(*shape):
+        return dma(2, *shape)
+
+    chunk = v((CH, DIM), F32)
+    four, eight, sixteen = (v((*n, CH, DIM), F32) for n in ((4,), (2, 4), (4, 4)))
+    image, text, own = (v((n, DIM), BF16) for n in (NI, NTX, ROWS))
+    image_sums, text_sums = v((NI, CH), F32), v((8, NTX), F32)
+    nr, nc = NI // CH, NTX // CH
+    pieces = both(4, 3)
     scratch = [
-        v((NI, DIM), BF16), v((NTX, DIM), BF16), v((8, BLK // CH, PIECE, CH), F32),
-        v((NI, CH), F32), v((NI, CH), F32), v((8, NTX), F32), v((8, NTX), F32), v((1, NTX), F32),
-        v((2, NTX // CH, CH, CH), F32), v((2, NI, CH), F32), v((CH, NTX), BF16), v((NI, CH), BF16),
-        v((4, 4, *chunk), F32), v((4, *chunk), F32), v((4, *chunk), F32), v((4, 4, *chunk), F32), v((2, 4, *chunk), F32), v((4, *chunk), F32),
-        v((ROWS, DIM), BF16), v((ROWS, DIM), BF16), v(chunk, F32), v((2, CUTS[1], DIM), F32),
-        v((NI // CH, CH), F32), v((3, NI // CH, CH), F32), v((NTX // CH, CH), F32), v((7, NTX // CH, CH), F32), v((6, 8, CH), F32), v((5, 8, CH), F32),
-        dma(2), dma(8), dma(2), dma(2), dma(2, 4),
-        dma(2, 6, 4), dma(2, 4, 4), dma(2, 3), dma(2, 7), dma(2, 5),
-        dma(2, 4, 3), dma(2, 4), dma(2, 4, 3), dma(2, 4, 4), dma(2, 4, 3), dma(2, 4), dma(2, 4, 3), dma(2, 2),
+        image, text, v((8, BLK // CH, PIECE, CH), F32),
+        image_sums, image_sums, text_sums, text_sums, v((1, NTX), F32),
+        v((2, nc, CH, CH), F32), v((2, NI, CH), F32), v((CH, NTX), BF16), v((NI, CH), BF16),
+        sixteen, four, four, sixteen, eight, four,
+        own, own, chunk, v((2, CUTS[1], DIM), F32),
+        v((nr, CH), F32), v((3, nr, CH), F32), v((nc, CH), F32), v((7, nc, CH), F32), v((6, 8, CH), F32), v((5, 8, CH), F32),
+        dma(2), dma(8), dma(2), dma(2), both(4),
+        both(6, 4), both(4, 4), both(3), both(7), both(5),
+        pieces, both(4), pieces, both(4, 4), pieces, both(4), pieces, both(2),
     ]
     shape = jax.ShapeDtypeStruct
     call = pl.pallas_call(

time: 185 us -> 184 us (level)
  no operation moved by 1% of the time
where the time goes in v5:
time: 184 us; the launch traced here: 183 us
  Pallas kernels  179 us (97%)
  between operations  4.75 us (3%)
    pallas_call x1, Pallas kernels, local(): loss, d_img, d_txt, dt, _ = call(log_scale.reshape(1), img, txt)  176 us

profile of v5, /device:TPU:0, one launch (start us, length us, event | category | flops | bytes accessed | tf_op | source)
XLA Modules:
  0.0 183.4 jit_solution(1115330874484486957)
XLA Ops:
  1.3 176.2 %clip.1 = (f32[1,1]{1,0:T(1,128)}, bf16[512,1024]{1,0:T(8,128)(2,1)}, bf16[512,1024]{1,0:T(8,128)(2,1)}, f32[1,1]{1,0:T(1,128)}, f32[32,2048,128]{2,1,0:T(8,128)}) custom-call(f32[1]{0:T(128)} %bitcast.3.t_ref, bf16[512,1024]{1,0:T(8,128)(2,1)} %img_ref.1, bf16[512,1024]{1,0:T(8,128)(2,1)} %txt_ref.1), custom_call_target="tpu_custom_call" | custom-call | tf_op jit(solution)/shard_map/clip/pallas_call | solution.py:621
  177.5 2.4 %hand_over.1 = (bf16[512,1024]{1,0:T(8,128)(2,1)}, bf16[512,1024]{1,0:T(8,128)(2,1)}) custom-call(bf16[512,1024]{1,0:T(8,128)(2,1)} %get-tuple-element.11.img_ref, bf16[512,1024]{1,0:T(8,128)(2,1)} %get-tuple-element.12.txt_ref), custom_call_target="tpu_custom_call" | custom-call | tf_op jit(solution)/shard_map/hand_over/pallas_call | solution.py:622
